TPU v7x, 128 devices: a whole 4x4x4 slice. The times are simulated.
128 devices in a mesh: tm: 16 (over y_hi, z, core), dp: 8 (over x, y_lo).
Axes of the slice: x: 4, y: 4 (y_hi: 2, y_lo: 2; y = y_hi * 2 + y_lo), z: 4, core: 2. Of those that a mesh axis runs over, the one named last changes fastest.
Arguments:
- encoded: bfloat16 [2048, 80, 1024], P('dp', 'tm'), may hold values from -6 to 6
- queries: bfloat16 [2048, 32, 1024], P(('dp', 'tm')), may hold values from -200 to 200
- cotangent: bfloat16 [2048, 32, 1024], P(('dp', 'tm')), may hold values from -0.044433594 to 0.044433594
- lengths: int32 [2048], P(('dp', 'tm')), may hold values from 2 to 80
- key_weight: bfloat16 [1024, 1024], replicated, may hold values from -0.1875 to 0.1875
- value_weight: bfloat16 [1024, 1024], replicated, may hold values from -0.1875 to 0.1875
Outputs:
- context: bfloat16 [2048, 32, 1024], P(('dp', 'tm'))
- key_grad: float32 [1024, 1024], replicated
- value_grad: float32 [1024, 1024], replicated
Inputs may be any that keep to these rules, and one draw needn't show every extreme that they name: Sequence b attends only to source positions below lengths[b].
All inputs are finite; a program needn't handle non-finite values.
Results may differ from a plain program's by a relative error of at most 0.0069.
Values may be sent and summed in bfloat16 or wider, within the bound.
A program may use at most 128 MiB of HBM per device.

v0:
```python
import math

import jax
import jax.numpy as jnp
from jax import lax
from jax.sharding import Mesh
from jax.sharding import PartitionSpec as P

TM = ("tm_0", "tm_1", "tm_2")
TM_DP = ("tm_0", "tm_1", "tm_2", "dp")
DP_TM = ("dp", "tm_0", "tm_1", "tm_2")


def in_blocks(x, dim, length):
    before, after = (x.shape[:dim], x.shape[dim + 1 :])
    return jnp.moveaxis(x.reshape(*before, length, -1, *after), dim, 0)


def laid_out(parts, dim):
    parts = jnp.moveaxis(parts, 0, dim)
    shape = parts.shape
    return parts.reshape(*shape[:dim], shape[dim] * shape[dim + 1], *shape[dim + 2 :])


def turned_blocks(parts, axes, order):
    shape = [lax.axis_size(a) for a in axes]
    parts = parts.reshape(*shape, *parts.shape[1:])
    for k in order:
        parts = lax.all_to_all(parts, axes[k], split_axis=k, concat_axis=k, tiled=True)
    return parts.reshape(-1, *parts.shape[len(axes) :])


def core_and_chips(x, groups, order, split_dim, concat_dim):
    length = lax.axis_size(groups[0]) * lax.axis_size(groups[1])
    parts = in_blocks(x, split_dim, length)
    return laid_out(turned_blocks(parts, groups, order), concat_dim)


def attend(queries, key_rows, value_rows, lengths, cotangent):
    score_scale = 1.0 / math.sqrt(queries.shape[-1])
    scores = (
        jnp.einsum("btd,bsd->bts", queries, key_rows, preferred_element_type=jnp.float32)
        * score_scale
    )
    positions = jnp.arange(key_rows.shape[1], dtype=jnp.int32)
    in_range = positions[None, None, :] < lengths[:, None, None]
    scores = jnp.where(in_range, scores, -1e30)
    row_max = jnp.max(scores, axis=-1, keepdims=True)
    weights = jnp.exp(scores - row_max)
    probabilities = weights / jnp.sum(weights, axis=-1, keepdims=True)
    probs_low = probabilities.astype(jnp.bfloat16)
    context = jnp.einsum(
        "bts,bsd->btd", probs_low, value_rows, preferred_element_type=jnp.float32
    ).astype(jnp.bfloat16)
    grad_probs = jnp.einsum(
        "btd,bsd->bts", cotangent, value_rows, preferred_element_type=jnp.float32
    )
    grad_scores = probabilities * (
        grad_probs - jnp.sum(probabilities * grad_probs, axis=-1, keepdims=True)
    )
    grad_low = grad_scores.astype(jnp.bfloat16)
    grad_values = jnp.einsum(
        "bts,btd->bsd", probs_low, cotangent, preferred_element_type=jnp.float32
    ).astype(jnp.bfloat16)
    grad_keys = (
        jnp.einsum("bts,btd->bsd", grad_low, queries, preferred_element_type=jnp.float32)
        * score_scale
    ).astype(jnp.bfloat16)
    return (context, grad_keys, grad_values)


def project(flattened, weight_matrix, shape):
    return (
        jnp.dot(flattened, weight_matrix, preferred_element_type=jnp.float32)
        .astype(jnp.bfloat16)
        .reshape(shape)
    )


def weight_term(flattened, gradient):
    model_width = flattened.shape[1]
    return lax.dot_general(
        flattened,
        gradient.reshape(-1, model_width),
        (((0,), (0,)), ((), ())),
        preferred_element_type=jnp.float32,
    )


def body(encoded, queries, cotangent, lengths, key_weight, value_weight):
    model_width = encoded.shape[2]
    regrouped = core_and_chips(encoded, (("tm_0", "tm_1"), "tm_2"), (1, 0), 0, 1)
    flattened = regrouped.reshape(-1, model_width)
    key_rows = project(flattened, key_weight, regrouped.shape)
    value_rows = project(flattened, value_weight, regrouped.shape)
    context, grad_keys, grad_values = attend(queries, key_rows, value_rows, lengths, cotangent)
    key_grad = weight_term(flattened, grad_keys)
    value_grad = weight_term(flattened, grad_values)
    key_grad, value_grad = lax.psum((key_grad, value_grad), TM_DP)
    return (context, key_grad, value_grad)


def solution(mesh):
    finer = Mesh(mesh.devices.reshape(2, 4, 2, mesh.shape["dp"]), ("tm_0", "tm_1", "tm_2", "dp"))
    return jax.shard_map(
        body,
        mesh=finer,
        in_specs=(
            P("dp", TM, None),
            P(DP_TM, None, None),
            P(DP_TM, None, None),
            P(DP_TM),
            P(),
            P(),
        ),
        out_specs=(P(DP_TM, None, None), P(), P()),
        check_vma=False,
    )
```

profile of v0, /device:TPU:1, one launch (start us, length us, event | category | flops | bytes accessed | tf_op | source)
XLA Modules:
  0.0 283.7 jit_solution(4655522840126873157)
XLA Ops:
  7.2 0.0 copy-start
  7.2 2.1 copy.17
  9.3 6.8 %all_to_all.10 = bf16[8,2,16,5,1024]{4,2,0,3,1:T(8,128)(2,1)S(1)} all-to-all(bf16[8,2,16,5,1024]{4,2,0,3,1:T(8,128)(2,1)S(1)} %copy.17), channel_id=1, replica_groups=mesh['tm_0'=2,'tm_1'=4,'tm_2'=2,'dp'=8] {'tm_2'}, dimensions={1} | all-to-all | bytes 5242880 | tf_op jit(solution)/shard_map/all_to_all | solution.py:29
  16.2 1.7 copy.18
  17.9 0.0 copy-start.5
  17.9 7.9 %all-to-all-start.1 = ((bf16[8,2,16,5,1024]{4,2,1,3,0:T(8,128)(2,1)}), bf16[8,2,16,5,1024]{4,2,1,3,0:T(8,128)(2,1)}, u32[]{:S(2)}, u32[]{:S(2)}) async-start(bf16[8,2,16,5,1024]{4,2,1,3,0:T(8,128)(2,1)} %copy.18), calls=%async_computation.1 | async-start | bytes 5242880 | tf_op jit(solution)/shard_map/all_to_all | solution.py:29
  25.8 0.0 all-reduce.3.cloned.1.call-start
  25.8 0.0 copy-done.5
  25.9 0.1 iota_compare_fusion
  25.9 31.8 %all-to-all-done.1 = bf16[8,2,16,5,1024]{4,2,1,3,0:T(8,128)(2,1)} async-done(((bf16[8,2,16,5,1024]{4,2,1,3,0:T(8,128)(2,1)}), bf16[8,2,16,5,1024]{4,2,1,3,0:T(8,128)(2,1)}, u32[]{:S(2)}, u32[]{:S(2)}) %all-to-all-start.1) | async-done | bytes 2621472 | tf_op jit(solution)/shard_map/all_to_all | solution.py:29
  57.7 2.0 copy.19
  59.7 3.6 %copy.20 = bf16[16,16,5,1024]{3,2,1,0:T(8,128)(2,1)} copy(bf16[16,16,5,1024]{3,0,2,1:T(8,128)(2,1)S(1)} %bitcast.35) | data formatting | bytes 5242880 | tf_op jit(solution)/shard_map/transpose | solution.py:20
  63.3 6.2 %reshape_reshape.7 = bf16[1280,1024]{1,0:T(8,128)(2,1)} reshape(bf16[16,16,5,1024]{3,2,1,0:T(8,128)(2,1)} %copy.20) | data formatting | bytes 5242880 | tf_op jit(solution)/shard_map/reshape;reshape | solution.py:93
  69.5 0.0 copy-done
  69.5 0.0 copy-start.3
  69.5 0.0 copy-start.6
  69.5 6.1 %convolution_convert_fusion = bf16[1280,1024]{1,0:T(8,128)(2,1)} fusion(bf16[1280,1024]{1,0:T(8,128)(2,1)} %reshape_reshape.7, bf16[1024,1024]{1,0:T(8,128)(2,1)S(1)} %copy-done), kind=kOutput, calls=%fused_computation.2 | convolution fusion | flops 2685665280 | bytes 7340032 | tf_op jit(solution)/shard_map/dot_general | solution.py:74
  75.7 0.0 copy-done.3
  75.7 0.0 copy-done.6
  75.7 0.0 copy-start.1
  75.7 3.1 %convolution_convert_fusion.1 = bf16[1280,1024]{1,0:T(8,128)(2,1)S(1)} fusion(bf16[1280,1024]{1,0:T(8,128)(2,1)S(1)} %copy-done.3, bf16[1024,1024]{1,0:T(8,128)(2,1)S(1)} %copy-done.6), kind=kOutput, calls=%fused_computation.3 | convolution fusion | flops 2685665280 | bytes 7340032 | tf_op jit(solution)/shard_map/dot_general | solution.py:74
  78.8 0.0 copy-done.1
  78.8 0.8 fusion.4
  79.6 0.9 fusion.8
  80.5 4.6 %convolution_convert_fusion.2 = bf16[16,80,1024]{2,1,0:T(8,128)(2,1)} fusion(bf16[16,32,1024]{2,1,0:T(8,128)(2,1)} %param.8, f32[16,32]{1,0:T(8,128)S(1)} %get-tuple-element.17, f32[16,32,80]{2,1,0:T(8,128)S(1)} %fusion.4), kind=kOutput, calls=%fused_computation.6 | convolution fusion | flops 85320272 | bytes 3835904 | tf_op jit(solution)/shard_map/bts,btd->bsd/dot_general | solution.py:62
  85.1 3.6 %multiply_reduce_fusion = (f32[16,32]{1,0:T(8,128)S(1)}, f32[16,32,80]{2,1,0:T(8,128)}) fusion(f32[16,32,80]{2,1,0:T(8,128)} %get-tuple-element.18, f32[16,32]{1,0:T(8,128)S(1)} %get-tuple-element.17, bf16[16,80,1024]{2,1,0:T(8,128)(2,1)} %bitcast.36, bf16[16,32,1024]{2,1,0:T(8,128)(2,1)} %param.8), kind=kOutput, calls=%fused_computation.15 | convolution fusion | flops 84008448 | bytes 4001792 | tf_op jit(solution)/shard_map/btd,bsd->bts/dot_general | solution.py:55
  88.7 4.1 %multiply_convert_fusion = bf16[16,80,1024]{2,1,0:T(8,128)(2,1)} fusion(bf16[16,32,1024]{2,1,0:T(8,128)(2,1)S(1)} %copy-done.1, f32[16,32,80]{2,1,0:T(8,128)} %get-tuple-element.20, f32[16,32]{1,0:T(8,128)S(1)} %get-tuple-element.19, f32[16,32]{1,0:T(8,128)S(1)} %get-tuple-element.17, f32[16,32,80]{2,1,0:T(8,128)S(1)} %fusion.4), kind=kOutput, calls=%fused_computation.1 | convolution fusion | flops 86712912 | bytes 4001792 | tf_op jit(solution)/shard_map/bts,btd->bsd/dot_general | solution.py:66
  92.8 0.0 copy-start.2
  92.8 0.0 copy-start.4
  92.8 7.6 %convolution_bitcast_fusion.1 = f32[1024,1024]{0,1:T(8,128)} fusion(bf16[1280,1024]{1,0:T(8,128)(2,1)} %bitcast.41, bf16[1280,1024]{1,0:T(8,128)(2,1)} %reshape_reshape.7), kind=kOutput, calls=%fused_computation.5 | convolution fusion | flops 2684354560 | bytes 9437184 | tf_op jit(solution)/shard_map/dot_general | solution.py:82
  100.4 0.0 copy-done.2
  100.5 0.0 copy-done.4
  100.5 4.4 %convolution_bitcast_fusion = f32[1024,1024]{0,1:T(8,128)} fusion(bf16[1280,1024]{1,0:T(8,128)(2,1)S(1)} %bitcast.38, bf16[1280,1024]{1,0:T(8,128)(2,1)S(1)} %copy-done.4), kind=kOutput, calls=%fused_computation.4 | convolution fusion | flops 2684354560 | bytes 9437184 | tf_op jit(solution)/shard_map/dot_general | solution.py:82
  104.9 0.0 all-reduce.3.cloned.1.call-update
  104.9 3.8 %convolution_convert_fusion.3 = bf16[16,32,1024]{2,1,0:T(8,128)(2,1)} fusion(bf16[16,80,1024]{2,1,0:T(8,128)(2,1)} %bitcast.37, f32[16,32]{1,0:T(8,128)S(1)} %get-tuple-element.17, f32[16,32,80]{2,1,0:T(8,128)S(1)} %fusion.4), kind=kOutput, calls=%fused_computation.7 | convolution fusion | flops 84533840 | bytes 3835904 | tf_op jit(solution)/shard_map/bts,bsd->btd/dot_general | solution.py:52
  108.7 157.4 %all-reduce.3.cloned.1.call-done = (f32[1024,1024]{0,1:T(8,128)}, f32[1024,1024]{0,1:T(8,128)}) async-done(((f32[1024,1024]{0,1:T(8,128)}, f32[1024,1024]{0,1:T(8,128)}), (f32[1024,1024]{0,1:T(8,128)}, f32[1024,1024]{0,1:T(8,128)})) %all-reduce.3.cloned.1.call-update) | async-done | bytes 8388624 | tf_op jit(solution)/shard_map/psum | solution.py:99
  266.2 5.3 %copy.21 = f32[1024,1024]{1,0:T(8,128)} copy(f32[1024,1024]{0,1:T(8,128)} %get-tuple-element.15) | data formatting | bytes 8388608
  271.5 5.3 %copy.22 = f32[1024,1024]{1,0:T(8,128)} copy(f32[1024,1024]{0,1:T(8,128)} %get-tuple-element.16) | data formatting | bytes 8388608
Async XLA Ops:
  7.2 62.4 %copy-start = (bf16[1024,1024]{1,0:T(8,128)(2,1)S(1)}, bf16[1024,1024]{1,0:T(8,128)(2,1)}, u32[]{:S(2)}) copy-start(bf16[1024,1024]{1,0:T(8,128)(2,1)} %param.11) | copy-start | bytes 6291460
  17.9 8.0 %copy-start.5 = (s32[16]{0:T(128)S(1)}, s32[16]{0:T(128)}, u32[]{:S(2)}) copy-start(s32[16]{0:T(128)} %param.9) | copy-start | bytes 196
  17.9 39.8 %all-to-all-start.1 = ((bf16[8,2,16,5,1024]{4,2,1,3,0:T(8,128)(2,1)}), bf16[8,2,16,5,1024]{4,2,1,3,0:T(8,128)(2,1)}, u32[]{:S(2)}, u32[]{:S(2)}) async-start(bf16[8,2,16,5,1024]{4,2,1,3,0:T(8,128)(2,1)} %copy.18), calls=%async_computation.1 | async-start | bytes 5242880 | tf_op jit(solution)/shard_map/all_to_all | solution.py:29
  25.8 240.4 %all-reduce.3.cloned.1.call-start = ((), (), s32[]{:S(2)}) async-start(), calls=%async_computation.2 | async-start | bytes 16777216 | tf_op jit(solution)/shard_map/psum | solution.py:99
  69.5 6.1 %copy-start.3 = (bf16[1280,1024]{1,0:T(8,128)(2,1)S(1)}, bf16[1280,1024]{1,0:T(8,128)(2,1)}, u32[]{:S(2)}) copy-start(bf16[1280,1024]{1,0:T(8,128)(2,1)} %reshape_reshape.7) | copy-start | bytes 7864324
  69.5 6.1 %copy-start.6 = (bf16[1024,1024]{1,0:T(8,128)(2,1)S(1)}, bf16[1024,1024]{1,0:T(8,128)(2,1)}, u32[]{:S(2)}) copy-start(bf16[1024,1024]{1,0:T(8,128)(2,1)} %param.10) | copy-start | bytes 6291460
  75.7 3.1 %copy-start.1 = (bf16[16,32,1024]{2,1,0:T(8,128)(2,1)S(1)}, bf16[16,32,1024]{2,1,0:T(8,128)(2,1)}, u32[]{:S(2)}) copy-start(bf16[16,32,1024]{2,1,0:T(8,128)(2,1)} %param.7) | copy-start | bytes 3145732
  92.8 7.6 %copy-start.2 = (bf16[16,80,1024]{2,1,0:T(8,128)(2,1)S(1)}, bf16[16,80,1024]{2,1,0:T(8,128)(2,1)}, u32[]{:S(2)}) copy-start(bf16[16,80,1024]{2,1,0:T(8,128)(2,1)} %convolution_convert_fusion.2) | copy-start | bytes 7864324
  92.8 7.6 %copy-start.4 = (bf16[1280,1024]{1,0:T(8,128)(2,1)S(1)}, bf16[1280,1024]{1,0:T(8,128)(2,1)}, u32[]{:S(2)}) copy-start(bf16[1280,1024]{1,0:T(8,128)(2,1)} %reshape_reshape.7) | copy-start | bytes 7864324
Sparse Core Ops, SparseCore 0:
  105.0 161.0 all-reduce.2
where the time goes:
time: 284 us
  waiting for transfers between devices  189 us (67%)
  matrix products  38.3 us (13%)
  local copies, waits for them, and re-layouts  26.4 us (9%)
  between operations  14.1 us (5%)
  starting transfers between devices  7.94 us (3%)
  blocking collectives  6.85 us (2%)
    psum x1, waiting for transfers between devices, body(): key_grad, value_grad = lax.psum((key_grad, value_grad), TM_DP)  157 us
    all_to_all x1, waiting for transfers between devices, turned_blocks(): lax.all_to_all(parts, axes[k], split_axis=k, concat_axis=k, tiled=True)  31.8 us
    dot_general x2, matrix products, weight_term(): lax.dot_general(flattened, gradient.reshape(-1, model_width), (((0,), (0,...  12.1 us
    unnamed x16, local copies, waits for them, and re-layouts  10.7 us
    dot_general x2, matrix products, project(): jnp.dot(flattened, weight_matrix, preferred_element_type=jnp.float32)  9.22 us
    all_to_all x1, starting transfers between devices, turned_blocks(): lax.all_to_all(parts, axes[k], split_axis=k, concat_axis=k, tiled=True)  7.91 us
    all_to_all x1, blocking collectives, turned_blocks(): lax.all_to_all(parts, axes[k], split_axis=k, concat_axis=k, tiled=True)  6.85 us
    another operation x1, local copies, waits for them, and re-layouts, body(): flattened = regrouped.reshape(-1, model_width)  6.23 us
  transfers between devices with their start and end apart: 2, of which 2 were waited for; matrix products, arithmetic and copies ran while one was open for 1% of the time, Pallas kernels for 0%

commit v1 on v0

v1 whole, which is shorter than its diff:
```python
import functools

import jax
import jax.numpy as jnp
from jax import lax
from jax.experimental import pallas as pl
from jax.experimental.pallas import tpu as pltpu
from jax.sharding import PartitionSpec as P

MESH = pl.DeviceIdType.MESH
F32, BF16 = jnp.float32, jnp.bfloat16
OFFS = (
    (0, 0, 0), (0, 0, 1),
    (0, 1, 0), (0, 3, 0), (1, 0, 0), (0, 1, 1), (0, 3, 1), (1, 0, 1),
    (1, 1, 0), (1, 3, 0), (0, 2, 0), (1, 1, 1), (1, 3, 1), (0, 2, 1),
    (1, 2, 0), (1, 2, 1),
)
GROUPS = ((0, 384, (0, 1, 2)), (384, 768, (1, 2, 0)), (768, 1024, (2, 0, 1)))
HOPS = (2, 1, 3)
SIZES = (256, 64, 16)


def nt(a, b):
    return lax.dot_general(a, b, (((1,), (1,)), ((), ())), preferred_element_type=F32)


def nn(a, b):
    return jnp.dot(a, b, preferred_element_type=F32)


def tn(a, b):
    return lax.dot_general(a, b, (((0,), (0,)), ((), ())), preferred_element_type=F32)


def kernel(
    enc, q, cot, lens, wk, wv, grads, ctx,
    e, et, v, st, gp, pg, qc, w, a, a_in, r_in, own, snd, rcv, rcv2, rcv3, res, ctxb,
    lsem, xs, xr, ds, dr, gs, gr, fs, fr, osem,
):
    tm, dp = lax.axis_index("tm"), lax.axis_index("dp")
    yh, z, c = tm // 8, (tm // 2) % 4, tm % 2
    x, y = dp // 2, yh * 2 + dp % 2
    at = (x, y, z)

    def device(x, y, z, c):
        return ((y // 2) * 8 + z * 2 + c, x * 2 + y % 2)

    def tm_at(off, sign):
        return ((yh + off[0]) % 2) * 8 + ((z + sign * off[1] + 4) % 4) * 2 + (c + off[2]) % 2

    def along(axis, hop):
        there = list(at)
        there[axis] = (there[axis] + hop) % 4
        return device(*there, c)

    partner = device(x, y, z, 1 - c)

    local = [
        pltpu.make_async_copy(q, qc.at[0], lsem.at[0]),
        pltpu.make_async_copy(cot, qc.at[1], lsem.at[1]),
        pltpu.make_async_copy(wk, w.at[0], lsem.at[2]),
        pltpu.make_async_copy(wv, w.at[1], lsem.at[3]),
        pltpu.make_async_copy(
            enc.at[:, pl.ds(pl.multiple_of(16 * tm, 16), 16)], e.at[pl.ds(0, 5)], lsem.at[4]
        ),
    ]
    barrier = pltpu.get_barrier_semaphore()
    peers = [(tm_at(off, 1), dp) for off in OFFS[1:]]
    peers += [along(0, h) for h in (1, 2, 3)] + [along(1, h) for h in (1, 3)]
    for peer in peers:
        pl.semaphore_signal(barrier, inc=1, device_id=peer, device_id_type=MESH)
    for copy in local:
        copy.start()
    pl.semaphore_wait(barrier, len(peers))

    def exchange(k, target):
        return pltpu.make_async_remote_copy(
            src_ref=enc.at[:, pl.ds(pl.multiple_of(16 * target, 16), 16)],
            dst_ref=e.at[pl.ds(5 * k, 5)],
            send_sem=xs.at[k],
            recv_sem=xr.at[k],
            device_id=(target, dp),
            device_id_type=MESH,
        )

    sends = []
    for k, off in enumerate(OFFS):
        if k:
            copy = exchange(k, tm_at(off, 1))
            copy.start()
            sends.append(copy)
    for copy in local[:2]:
        copy.wait()

    def to_partner(src, dst, k):
        return pltpu.make_async_remote_copy(
            src_ref=src, dst_ref=dst, send_sem=ds.at[k], recv_sem=dr.at[k],
            device_id=partner, device_id_type=MESH,
        )

    operand = to_partner(qc.at[1 - c], r_in, 0)
    operand.start()
    sends.append(operand)

    column = lax.broadcasted_iota(jnp.int32, (1, 512), 1) // 32
    limit = jnp.zeros((1, 512), jnp.int32)
    for b in range(16):
        limit = jnp.where(column == b, lens[b], limit)
    row = lax.broadcasted_iota(jnp.int32, (80, 512), 0)
    same = row % 16 == column
    for k, off in enumerate(OFFS):
        position = 5 * tm_at(off, -1) + row // 16
        st[pl.ds(80 * k, 80), :] = jnp.where(same & (position < limit), 0.0, -1e30)

    for copy in local[2:]:
        copy.wait()

    def arrive(j, carry):
        top, total, dots = carry
        for i in range(3):
            k = 3 * j + 1 + i
            pltpu.make_async_remote_copy(
                src_ref=enc.at[:, pl.ds(0, 16)],
                dst_ref=e.at[pl.ds(5 * k, 5)],
                send_sem=xs.at[k],
                recv_sem=xr.at[k],
                device_id=partner,
                device_id_type=MESH,
            ).wait_recv()
        rows = pl.ds(pl.multiple_of(256 * j, 256), 256)
        block = e[pl.ds(16 * j, 16)].reshape(256, 1024)
        et[:, rows] = block.T
        keys = nn(block, w[0]).astype(BF16)
        values = nn(block, w[1]).astype(BF16)
        v[rows, :] = values
        scores = nt(keys, qc[0]) * (1.0 / 32.0) + st[rows, :]
        st[rows, :] = scores
        slope = nt(values, qc[1])
        gp[rows, :] = slope
        scores = scores.reshape(32, 8, 512)
        peak = jnp.maximum(top, jnp.max(scores, axis=0))
        weights = jnp.exp(scores - peak)
        shrink = jnp.exp(top - peak)
        total = total * shrink + jnp.sum(weights, axis=0)
        dots = dots * shrink + jnp.sum(weights * slope.reshape(32, 8, 512), axis=0)
        return peak, total, dots

    zero = jnp.zeros((8, 512), F32)
    top, total, dots = lax.fori_loop(0, 5, arrive, (jnp.full((8, 512), -1e30, F32), zero, zero))
    peak = jnp.max(top, axis=0, keepdims=True)
    shrink = jnp.exp(top - peak)
    scale = 1.0 / jnp.sum(total * shrink, axis=0, keepdims=True)
    mean = jnp.sum(dots * shrink, axis=0, keepdims=True) * scale

    def normalise(j, carry):
        rows = pl.ds(pl.multiple_of(128 * j, 128), 128)
        probs = jnp.exp(st[rows, :] - peak) * scale
        pg[1, rows, :] = probs.astype(BF16)
        pg[0, rows, :] = (probs * (gp[rows, :] - mean)).astype(BF16)
        return carry

    lax.fori_loop(0, 10, normalise, 0)

    def gather_rows(slot):
        factor = jnp.where(slot == 0, 1.0 / 32.0, 1.0)

        def one(j, carry):
            rows = pl.ds(pl.multiple_of(256 * j, 256), 256)
            a[slot, rows, :] = (nn(et[rows, :], pg[slot]) * factor).astype(BF16)
            return carry

        lax.fori_loop(0, 4, one, 0)

    gather_rows(1 - c)
    operand2 = to_partner(a.at[1 - c], a_in, 1)
    operand2.start()
    sends.append(operand2)
    gather_rows(c)
    operand.wait_recv()
    operand2.wait_recv()

    def hop_copy(g, phase, h, src, dst):
        axis = GROUPS[g][2][phase if phase < 3 else 5 - phase]
        copy = pltpu.make_async_remote_copy(
            src_ref=src, dst_ref=dst, send_sem=gs.at[g, phase, h], recv_sem=gr.at[g, phase, h],
            device_id=along(axis, HOPS[h]), device_id_type=MESH,
        )
        return copy

    def turned(axis, hop, size):
        return pl.multiple_of(((at[axis] + hop) % 4) * size, size)

    copies = {}
    for h in range(4):
        for g, (lo, hi, order) in enumerate(GROUPS):
            hop = HOPS[h] if h < 3 else 0
            rows = pl.ds(turned(order[0], hop, 256), 256)
            term = nn(a[c, rows, :], qc[c, :, lo:hi]) + nn(a_in[rows, :], r_in[:, lo:hi])
            if h < 3:
                snd[h, :, lo:hi] = term.astype(BF16)
                copy = hop_copy(g, 0, h, snd.at[h, :, pl.ds(lo, hi - lo)], rcv.at[h, :, pl.ds(lo, hi - lo)])
                copy.start()
                sends.append(copy)
                copies[g, 0, h] = copy
            else:
                own[:, lo:hi] = term

    for j in range(2):
        ctxb[pl.ds(256 * j, 256), :] = tn(pg[1, :, pl.ds(256 * j, 256)], v[...]).astype(BF16)
    out_ctx = pltpu.make_async_copy(ctxb, ctx, osem.at[0])
    out_ctx.start()

    for phase in (1, 2):
        size = SIZES[phase - 1]
        less = SIZES[phase]
        into, outof = (rcv, rcv2) if phase == 1 else (rcv2, rcv3)
        for g, (lo, hi, order) in enumerate(GROUPS):
            for h in range(3):
                copies[g, phase - 1, h].wait_recv()
            sums = own[0:size, lo:hi]
            for h in range(3):
                sums = sums + into[h, :, lo:hi].astype(F32)
            own[0:size, lo:hi] = sums
            snd[2 + phase, 0:size, lo:hi] = sums.astype(BF16)
            for h in range(3):
                rows = pl.ds(turned(order[phase], HOPS[h], less), less)
                src = snd.at[2 + phase, rows, pl.ds(lo, hi - lo)]
                copy = hop_copy(g, phase, h, src, outof.at[h, :, pl.ds(lo, hi - lo)])
                copy.start()
                sends.append(copy)
                copies[g, phase, h] = copy
            keep = own[pl.ds(turned(order[phase], 0, less), less), lo:hi]
            own[0:less, lo:hi] = keep

    for g, (lo, hi, order) in enumerate(GROUPS):
        for h in range(3):
            copies[g, 2, h].wait_recv()
        sums = own[0:16, lo:hi]
        for h in range(3):
            sums = sums + rcv3[h, :, lo:hi].astype(F32)
        first = at[order[0]] * 256 + at[order[1]] * 64 + at[order[2]] * 16
        res[c, pl.ds(pl.multiple_of(first, 16), 16), lo:hi] = sums.astype(BF16)
    blocks = {}
    for phase in (3, 4, 5):
        depth = 5 - phase
        size = SIZES[depth]
        for g, (lo, hi, order) in enumerate(GROUPS):
            if phase > 3:
                for h in range(3):
                    copies[g, phase - 1, h].wait_recv()
            first = sum(at[order[i]] * SIZES[i] for i in range(depth + 1))
            block = res.at[c, pl.ds(pl.multiple_of(first, size), size), pl.ds(lo, hi - lo)]
            for h in range(3):
                copy = hop_copy(g, phase, h, block, block)
                copy.start()
                sends.append(copy)
                copies[g, phase, h] = copy
    forwards = []
    for h in (3, 1, 2, 0):
        for g, (lo, hi, order) in enumerate(GROUPS):
            hop = HOPS[h] if h < 3 else 0
            if h < 3:
                copies[g, 5, h].wait_recv()
            rows = pl.ds(turned(order[0], 4 - hop, 256), 256)
            block = res.at[c, rows, pl.ds(lo, hi - lo)]
            copy = pltpu.make_async_remote_copy(
                src_ref=block, dst_ref=block, send_sem=fs.at[g, h], recv_sem=fr.at[g, h],
                device_id=partner, device_id_type=MESH,
            )
            copy.start()
            sends.append(copy)
            forwards.append(copy)
    for copy in forwards:
        copy.wait_recv()
    out = pltpu.make_async_copy(res, grads, osem.at[1])
    out.start()
    for copy in sends:
        copy.wait_send()
    out_ctx.wait()
    out.wait()


def body(encoded, queries, cotangent, lengths, key_weight, value_weight):
    any_space = pl.BlockSpec(memory_space=pltpu.HBM)
    dma = pltpu.SemaphoreType.DMA
    grads, context = pl.pallas_call(
        kernel,
        out_shape=(
            jax.ShapeDtypeStruct((2, 1024, 1024), BF16),
            jax.ShapeDtypeStruct((512, 1024), BF16),
        ),
        in_specs=[any_space] * 3 + [pl.BlockSpec(memory_space=pltpu.SMEM)] + [any_space] * 2,
        out_specs=(any_space, any_space),
        scratch_shapes=[
            pltpu.VMEM((80, 16, 1024), BF16),
            pltpu.VMEM((1024, 1280), BF16),
            pltpu.VMEM((1280, 1024), BF16),
            pltpu.VMEM((1280, 512), F32),
            pltpu.VMEM((1280, 512), F32),
            pltpu.VMEM((2, 1280, 512), BF16),
            pltpu.VMEM((2, 512, 1024), BF16),
            pltpu.VMEM((2, 1024, 1024), BF16),
            pltpu.VMEM((2, 1024, 512), BF16),
            pltpu.VMEM((1024, 512), BF16),
            pltpu.VMEM((512, 1024), BF16),
            pltpu.VMEM((256, 1024), F32),
            pltpu.VMEM((5, 256, 1024), BF16),
            pltpu.VMEM((3, 256, 1024), BF16),
            pltpu.VMEM((3, 64, 1024), BF16),
            pltpu.VMEM((3, 16, 1024), BF16),
            pltpu.VMEM((2, 1024, 1024), BF16),
            pltpu.VMEM((512, 1024), BF16),
            dma((5,)), dma((16,)), dma((16,)), dma((2,)), dma((2,)),
            dma((3, 6, 3)), dma((3, 6, 3)), dma((3, 4)), dma((3, 4)), dma((2,)),
        ],
        compiler_params=pltpu.CompilerParams(
            collective_id=0, has_side_effects=True, vmem_limit_bytes=60 * 2**20
        ),
    )(
        jnp.transpose(encoded, (1, 0, 2)),
        queries.reshape(512, 1024),
        cotangent.reshape(512, 1024),
        lengths,
        key_weight,
        value_weight,
    )
    return context.reshape(16, 32, 1024), grads[0].astype(F32), grads[1].astype(F32)


def solution(mesh):
    return jax.shard_map(
        body,
        mesh=mesh,
        in_specs=(
            P("dp", "tm", None),
            P(("dp", "tm"), None, None),
            P(("dp", "tm"), None, None),
            P(("dp", "tm")),
            P(),
            P(),
        ),
        out_specs=(P(("dp", "tm"), None, None), P(), P()),
        check_vma=False,
    )
```

time: 284 us -> 101 us (0.36)
  waiting for transfers between devices: 189 us -> 0 us
  Pallas kernels: 0 us -> 92.9 us
  matrix products: 38.3 us -> 0 us
  local copies, waits for them, and re-layouts: 26.4 us -> 0.97 us
  between operations: 14.1 us -> 0.65 us
  starting transfers between devices: 7.94 us -> 0 us
  blocking collectives: 6.85 us -> 0 us
  other arithmetic: 0.94 us -> 6.75 us
    psum x1 -> x0, waiting for transfers between devices: 157 us -> none  [body(): key_grad, value_grad = lax.psum((key_grad, value_grad), TM_DP)]
    pallas_call x0 -> x1, Pallas kernels: none -> 92.9 us  [body(): pl.pallas_call(kernel, out_shape=(jax.ShapeDtypeStruct((2, 1024, 1024), B...]
    dot_general x9 -> x0, matrix products: 38.3 us -> none  [the longest x2 12.1 us: weight_term(): lax.dot_general(flattened, gradient.reshape(-1, model_width), (((0,), (0,...]
    all_to_all x1 -> x0, waiting for transfers between devices: 31.8 us -> none  [turned_blocks(): lax.all_to_all(parts, axes[k], split_axis=k, concat_axis=k, tiled=True)]
    unnamed x16 -> x3, local copies, waits for them, and re-layouts: 10.7 us -> 0.97 us
    another operation x2 -> x0, local copies, waits for them, and re-layouts: 8.36 us -> none  [the longest x1 6.23 us: body(): flattened = regrouped.reshape(-1, model_width)]
    all_to_all x1 -> x0, starting transfers between devices: 7.91 us -> none  [turned_blocks(): lax.all_to_all(parts, axes[k], split_axis=k, concat_axis=k, tiled=True)]
    all_to_all x1 -> x0, blocking collectives: 6.85 us -> none  [turned_blocks(): lax.all_to_all(parts, axes[k], split_axis=k, concat_axis=k, tiled=True)]
  transfers between devices with their start and end apart: 2 -> 0, of which waited for: 2 -> 0; matrix products, arithmetic and copies ran while one was open for 1% -> 0% of each run, Pallas kernels for 0% -> 0%
where the time goes in v1:
time: 101 us
  Pallas kernels  92.9 us (92%)
  other arithmetic  6.75 us (7%)
    pallas_call x1, Pallas kernels, body(): pl.pallas_call(kernel, out_shape=(jax.ShapeDtypeStruct((2, 1024, 1024), B...  92.9 us
    convert_element_type x1, other arithmetic, body(): grads[1].astype(F32)  6.75 us

profile of v1, /device:TPU:1, one launch (start us, length us, event | category | flops | bytes accessed | tf_op | source)
XLA Modules:
  0.0 101.3 jit_solution(8541725654027109570)
XLA Ops:
  0.6 92.9 %shard_map.85 = (bf16[2,1024,1024]{2,1,0:T(8,128)(2,1)}, bf16[512,1024]{1,0:T(8,128)(2,1)}) custom-call(bf16[5,256,1024]{2,1,0:T(8,128)(2,1)} %bitcast.10, bf16[512,1024]{1,0:T(8,128)(2,1)} %bitcast.11, bf16[512,1024]{1,0:T(8,128)(2,1)} %bitcast.12, s32[16]{0:T(128)} %lens.1, bf16[1024,1024]{1,0:T(8,128)(2,1)} %wk.1, bf16[1024,1024]{1,0:T(8,128)(2,1)} %wv.1), custom_call_target="tpu_custom_call" | custom-call | tf_op jit(solution)/shard_map/pallas_call | solution.py:286
  93.5 0.0 copy-start
  93.5 6.8 %bitcast_convert_fusion = (f32[1024,1024]{1,0:T(8,128)}, f32[1024,1024]{1,0:T(8,128)}) fusion(bf16[2,1024,1024]{2,1,0:T(8,128)(2,1)} %get-tuple-element.6), kind=kLoop, calls=%fused_computation | loop fusion | flops 2097152 | bytes 12582912 | tf_op jit(solution)/shard_map/convert_element_type | solution.py:327
  100.3 0.0 copy-done
  100.3 1.0 copy.10
Async XLA Ops:
  93.5 6.8 %copy-start = (bf16[512,1024]{1,0:T(8,128)(2,1)S(1)}, bf16[512,1024]{1,0:T(8,128)(2,1)}, u32[]{:S(2)}) copy-start(bf16[512,1024]{1,0:T(8,128)(2,1)} %get-tuple-element.5) | copy-start | bytes 3145732

commit v2 on v1

--- a/solution.py
+++ b/solution.py
@@ -33,9 +33,9 @@
 
 
 def kernel(
-    enc, q, cot, lens, wk, wv, grads, ctx,
-    e, et, v, st, gp, pg, qc, w, a, a_in, r_in, own, snd, rcv, rcv2, rcv3, res, ctxb,
-    lsem, xs, xr, ds, dr, gs, gr, fs, fr, osem,
+    enc, q, cot, lens, wk, wv, res, ctx,
+    e, et, v, st, gp, pg, qc, w, a, a_in, r_in, own, snd, rcv, rcv2, rcv3,
+    lsem, xs, xr, ds, dr, gs, gr, fs, fr,
 ):
     tm, dp = lax.axis_index("tm"), lax.axis_index("dp")
     yh, z, c = tm // 8, (tm // 2) % 4, tm % 2
@@ -206,9 +206,7 @@
                 own[:, lo:hi] = term
 
     for j in range(2):
-        ctxb[pl.ds(256 * j, 256), :] = tn(pg[1, :, pl.ds(256 * j, 256)], v[...]).astype(BF16)
-    out_ctx = pltpu.make_async_copy(ctxb, ctx, osem.at[0])
-    out_ctx.start()
+        ctx[pl.ds(256 * j, 256), :] = tn(pg[1, :, pl.ds(256 * j, 256)], v[...]).astype(BF16)
 
     for phase in (1, 2):
         size = SIZES[phase - 1]
@@ -240,7 +238,6 @@
             sums = sums + rcv3[h, :, lo:hi].astype(F32)
         first = at[order[0]] * 256 + at[order[1]] * 64 + at[order[2]] * 16
         res[c, pl.ds(pl.multiple_of(first, 16), 16), lo:hi] = sums.astype(BF16)
-    blocks = {}
     for phase in (3, 4, 5):
         depth = 5 - phase
         size = SIZES[depth]
@@ -272,12 +269,22 @@
             forwards.append(copy)
     for copy in forwards:
         copy.wait_recv()
-    out = pltpu.make_async_copy(res, grads, osem.at[1])
-    out.start()
     for copy in sends:
         copy.wait_send()
-    out_ctx.wait()
-    out.wait()
+
+
+def finish(sums, context, key_grad, value_grad, context_out, wide, sem):
+    copies = [pltpu.make_async_copy(context, context_out, sem.at[8])]
+    copies[0].start()
+    for i, out in enumerate((key_grad, value_grad)):
+        for j in range(4):
+            rows = pl.ds(256 * j, 256)
+            wide[i, rows, :] = sums[i, rows, :].astype(F32)
+            copy = pltpu.make_async_copy(wide.at[i, rows], out.at[rows], sem.at[4 * i + j])
+            copy.start()
+            copies.append(copy)
+    for copy in copies:
+        copy.wait()
 
 
 def body(encoded, queries, cotangent, lengths, key_weight, value_weight):
@@ -286,11 +293,11 @@
     grads, context = pl.pallas_call(
         kernel,
         out_shape=(
-            jax.ShapeDtypeStruct((2, 1024, 1024), BF16),
-            jax.ShapeDtypeStruct((512, 1024), BF16),
+            pltpu.VMEM((2, 1024, 1024), BF16),
+            pltpu.VMEM((512, 1024), BF16),
         ),
         in_specs=[any_space] * 3 + [pl.BlockSpec(memory_space=pltpu.SMEM)] + [any_space] * 2,
-        out_specs=(any_space, any_space),
+        out_specs=(pl.BlockSpec(memory_space=pltpu.VMEM), pl.BlockSpec(memory_space=pltpu.VMEM)),
         scratch_shapes=[
             pltpu.VMEM((80, 16, 1024), BF16),
             pltpu.VMEM((1024, 1280), BF16),
@@ -308,13 +315,11 @@
             pltpu.VMEM((3, 256, 1024), BF16),
             pltpu.VMEM((3, 64, 1024), BF16),
             pltpu.VMEM((3, 16, 1024), BF16),
-            pltpu.VMEM((2, 1024, 1024), BF16),
-            pltpu.VMEM((512, 1024), BF16),
             dma((5,)), dma((16,)), dma((16,)), dma((2,)), dma((2,)),
-            dma((3, 6, 3)), dma((3, 6, 3)), dma((3, 4)), dma((3, 4)), dma((2,)),
+            dma((3, 6, 3)), dma((3, 6, 3)), dma((3, 4)), dma((3, 4)),
         ],
         compiler_params=pltpu.CompilerParams(
-            collective_id=0, has_side_effects=True, vmem_limit_bytes=60 * 2**20
+            collective_id=0, has_side_effects=True, vmem_limit_bytes=50 * 2**20
         ),
     )(
         jnp.transpose(encoded, (1, 0, 2)),
@@ -324,7 +329,19 @@
         key_weight,
         value_weight,
     )
-    return context.reshape(16, 32, 1024), grads[0].astype(F32), grads[1].astype(F32)
+    key_grad, value_grad, context = pl.pallas_call(
+        finish,
+        out_shape=(
+            jax.ShapeDtypeStruct((1024, 1024), F32),
+            jax.ShapeDtypeStruct((1024, 1024), F32),
+            jax.ShapeDtypeStruct((512, 1024), BF16),
+        ),
+        in_specs=[pl.BlockSpec(memory_space=pltpu.VMEM)] * 2,
+        out_specs=(any_space,) * 3,
+        scratch_shapes=[pltpu.VMEM((2, 1024, 1024), F32), dma((9,))],
+        compiler_params=pltpu.CompilerParams(vmem_limit_bytes=16 * 2**20),
+    )(grads, context)
+    return context.reshape(16, 32, 1024), key_grad, value_grad
 
 
 def solution(mesh):

time: 101 us -> 95.5 us (0.946)
  other arithmetic: 6.75 us -> 0 us
  Pallas kernels: 92.9 us -> 94.8 us
    convert_element_type x1 -> x0, other arithmetic: 6.75 us -> none  [body(): grads[1].astype(F32)]
    pallas_call x1 -> x2, Pallas kernels: 92.9 us -> 94.8 us  [the longest x1 91.1 us: body(): pl.pallas_call(kernel, out_shape=(pltpu.VMEM((2, 1024, 1024), BF16), pltp...]
where the time goes in v2:
time: 95.5 us; the launch traced here: 95.4 us
  Pallas kernels  94.8 us (99%)
    pallas_call x1, Pallas kernels, body(): pl.pallas_call(kernel, out_shape=(pltpu.VMEM((2, 1024, 1024), BF16), pltp...  91.1 us
    pallas_call x1, Pallas kernels, body(): pl.pallas_call(finish, out_shape=(jax.ShapeDtypeStruct((1024, 1024), F32)...  3.69 us

profile of v2, /device:TPU:1, one launch (start us, length us, event | category | flops | bytes accessed | tf_op | source)
XLA Modules:
  0.0 95.4 jit_solution(16140112911243962995)
XLA Ops:
  0.6 91.1 %shard_map.85 = (bf16[2,1024,1024]{2,1,0:T(8,128)(2,1)S(1)}, bf16[512,1024]{1,0:T(8,128)(2,1)S(1)}) custom-call(bf16[5,256,1024]{2,1,0:T(8,128)(2,1)} %bitcast.4, bf16[512,1024]{1,0:T(8,128)(2,1)} %bitcast.5, bf16[512,1024]{1,0:T(8,128)(2,1)} %bitcast.6, s32[16]{0:T(128)} %lens.1, bf16[1024,1024]{1,0:T(8,128)(2,1)} %wk.1, bf16[1024,1024]{1,0:T(8,128)(2,1)} %wv.1), custom_call_target="tpu_custom_call" | custom-call | tf_op jit(solution)/shard_map/pallas_call | solution.py:293
  91.7 3.7 %shard_map.86 = (f32[1024,1024]{1,0:T(8,128)}, f32[1024,1024]{1,0:T(8,128)}, bf16[512,1024]{1,0:T(8,128)(2,1)}) custom-call(bf16[2,1024,1024]{2,1,0:T(8,128)(2,1)S(1)} %get-tuple-element.8.sums, bf16[512,1024]{1,0:T(8,128)(2,1)S(1)} %get-tuple-element.9.context), custom_call_target="tpu_custom_call" | custom-call | tf_op jit(solution)/shard_map/pallas_call | solution.py:332

commit v3 on v2

v3 whole, which is shorter than its diff:
```python
import functools

import jax
import jax.numpy as jnp
from jax import lax
from jax.experimental import pallas as pl
from jax.experimental.pallas import tpu as pltpu
from jax.sharding import PartitionSpec as P

MESH = pl.DeviceIdType.MESH
F32, BF16 = jnp.float32, jnp.bfloat16
OFFS = (
    (0, 0, 0), (0, 0, 1),
    (0, 1, 0), (0, 3, 0), (1, 0, 0), (0, 1, 1), (0, 3, 1), (1, 0, 1),
    (1, 1, 0), (1, 3, 0), (0, 2, 0), (1, 1, 1), (1, 3, 1), (0, 2, 1),
    (1, 2, 0), (1, 2, 1),
)
FLOWS = (
    (0, 256, (0, 1, 2)), (256, 384, (1, 2, 0)), (384, 512, (2, 0, 1)),
    (512, 768, (2, 0, 1)), (768, 896, (0, 1, 2)), (896, 1024, (1, 2, 0)),
)
PARTS = ((0, 1, 2), (3, 4, 5))
HOPS = (2, 1, 3)


def nt(a, b):
    return lax.dot_general(a, b, (((1,), (1,)), ((), ())), preferred_element_type=F32)


def nn(a, b):
    return jnp.dot(a, b, preferred_element_type=F32)


def tn(a, b):
    return lax.dot_general(a, b, (((0,), (0,)), ((), ())), preferred_element_type=F32)


def kernel(
    enc, q, cot, lens, wk, wv, res, ctx,
    e, et, v, st, gp, pg, qc, w, a, a_out, r, part, own, snd, snd2, rcv, rcv2, last_sums,
    lsem, xs, xr, ds, dr, gs, gr, fs, fr,
):
    tm, dp = lax.axis_index("tm"), lax.axis_index("dp")
    yh, z, c = tm // 8, (tm // 2) % 4, tm % 2
    x, y = dp // 2, yh * 2 + dp % 2
    at = (x, y, z)

    def device(x, y, z, c):
        return ((y // 2) * 8 + z * 2 + c, x * 2 + y % 2)

    def tm_at(off, sign):
        return ((yh + off[0]) % 2) * 8 + ((z + sign * off[1] + 4) % 4) * 2 + (c + off[2]) % 2

    def along(axis, hop):
        there = list(at)
        there[axis] = (there[axis] + hop) % 4
        return device(*there, c)

    partner = device(x, y, z, 1 - c)

    local = [
        pltpu.make_async_copy(q, qc.at[0], lsem.at[0]),
        pltpu.make_async_copy(cot, qc.at[1], lsem.at[1]),
        pltpu.make_async_copy(wk, w.at[0], lsem.at[2]),
        pltpu.make_async_copy(wv, w.at[1], lsem.at[3]),
        pltpu.make_async_copy(
            enc.at[:, pl.ds(pl.multiple_of(16 * tm, 16), 8)], e.at[0, pl.ds(0, 5)], lsem.at[4]
        ),
        pltpu.make_async_copy(
            enc.at[:, pl.ds(pl.multiple_of(16 * tm + 8, 8), 8)], e.at[1, pl.ds(0, 5)], lsem.at[5]
        ),
    ]
    barrier = pltpu.get_barrier_semaphore()
    peers = [(tm_at(off, 1), dp) for off in OFFS[1:]]
    peers += [along(0, h) for h in (1, 2, 3)] + [along(1, h) for h in (1, 3)]
    for peer in peers:
        pl.semaphore_signal(barrier, inc=1, device_id=peer, device_id_type=MESH)
    for copy in local:
        copy.start()
    pl.semaphore_wait(barrier, len(peers))

    def exchange(h, k, target):
        return pltpu.make_async_remote_copy(
            src_ref=enc.at[:, pl.ds(pl.multiple_of(16 * target + 8 * h, 8), 8)],
            dst_ref=e.at[h, pl.ds(5 * k, 5)],
            send_sem=xs.at[h, k],
            recv_sem=xr.at[h, k],
            device_id=(target, dp),
            device_id_type=MESH,
        )

    sends = []
    for h in range(2):
        for k, off in enumerate(OFFS):
            if k:
                copy = exchange(h, k, tm_at(off, 1))
                copy.start()
                sends.append(copy)
    for copy in local[:2]:
        copy.wait()

    def to_partner(src, dst, k):
        return pltpu.make_async_remote_copy(
            src_ref=src, dst_ref=dst, send_sem=ds.at[k], recv_sem=dr.at[k],
            device_id=partner, device_id_type=MESH,
        )

    operands = []
    for h in range(2):
        half = pl.ds(256 * h, 256)
        copy = to_partner(qc.at[1 - c, half], r.at[h, pl.ds(256, 256)], h)
        copy.start()
        sends.append(copy)
        operands.append(copy)
        copy = pltpu.make_async_copy(qc.at[c, half], r.at[h, pl.ds(0, 256)], lsem.at[6 + h])
        copy.start()
        local.append(copy)

    column = lax.broadcasted_iota(jnp.int32, (1, 256), 1) // 32
    row = lax.broadcasted_iota(jnp.int32, (40, 256), 0)
    same = row % 8 == column
    for h in range(2):
        limit = jnp.zeros((1, 256), jnp.int32)
        for b in range(8):
            limit = jnp.where(column == b, lens[8 * h + b], limit)
        for k, off in enumerate(OFFS):
            position = 5 * tm_at(off, -1) + row // 8
            st[h, pl.ds(40 * k, 40), :] = jnp.where(same & (position < limit), 0.0, -1e30)

    for copy in local[2:]:
        copy.wait()

    def stream(h):
        def arrive(j, carry):
            top, total, dots = carry
            for i in range(3):
                k = 3 * j + 1 + i
                pltpu.make_async_remote_copy(
                    src_ref=enc.at[:, pl.ds(0, 8)],
                    dst_ref=e.at[h, pl.ds(5 * k, 5)],
                    send_sem=xs.at[h, k],
                    recv_sem=xr.at[h, k],
                    device_id=partner,
                    device_id_type=MESH,
                ).wait_recv()
            rows = pl.ds(pl.multiple_of(128 * j, 128), 128)
            block = e[h, pl.ds(16 * j, 16)].reshape(128, 1024)
            et[h, :, rows] = block.T
            keys = nn(block, w[0]).astype(BF16)
            values = nn(block, w[1]).astype(BF16)
            v[h, rows, :] = values
            scores = nt(keys, qc[0, pl.ds(256 * h, 256)]) * (1.0 / 32.0) + st[h, rows, :]
            st[h, rows, :] = scores
            slope = nt(values, qc[1, pl.ds(256 * h, 256)])
            gp[h, rows, :] = slope
            scores = scores.reshape(16, 8, 256)
            peak = jnp.maximum(top, jnp.max(scores, axis=0))
            weights = jnp.exp(scores - peak)
            shrink = jnp.exp(top - peak)
            total = total * shrink + jnp.sum(weights, axis=0)
            dots = dots * shrink + jnp.sum(weights * slope.reshape(16, 8, 256), axis=0)
            return peak, total, dots

        zero = jnp.zeros((8, 256), F32)
        top, total, dots = lax.fori_loop(0, 5, arrive, (jnp.full((8, 256), -1e30, F32), zero, zero))
        peak = jnp.max(top, axis=0, keepdims=True)
        shrink = jnp.exp(top - peak)
        scale = 1.0 / jnp.sum(total * shrink, axis=0, keepdims=True)
        mean = jnp.sum(dots * shrink, axis=0, keepdims=True) * scale

        def normalise(j, carry):
            rows = pl.ds(pl.multiple_of(128 * j, 128), 128)
            probs = jnp.exp(st[h, rows, :] - peak) * scale
            pg[h, 1, rows, :] = probs.astype(BF16)
            pg[h, 0, rows, :] = (probs * (gp[h, rows, :] - mean)).astype(BF16)
            return carry

        lax.fori_loop(0, 5, normalise, 0)

    def weigh(h, slot):
        factor = jnp.where(slot == 0, 1.0 / 32.0, 1.0)
        return (nn(et[h], pg[h, slot]) * factor).astype(BF16)

    def swap(h):
        a_out[h] = weigh(h, 1 - c)
        copy = to_partner(a_out.at[h], a.at[h, :, pl.ds(256, 256)], 2 + h)
        copy.start()
        sends.append(copy)
        a[h, :, 0:256] = weigh(h, c)
        operands[h].wait_recv()
        return copy

    stream(0)
    swap(0).wait_recv()
    def first_half(j, carry):
        rows = pl.ds(pl.multiple_of(256 * j, 256), 256)
        part[rows, :] = nn(a[0, rows, :], r[0])
        return carry

    lax.fori_loop(0, 4, first_half, 0)
    stream(1)
    last = swap(1)
    last.wait_recv()

    def pick(axis, value):
        return value[axis] * (1 - c) + value[(axis + 1) % 3] * c

    def there(axis, hop):
        place = [
            (at[i] + hop * ((1 - c) if i == axis else c if i == (axis + 1) % 3 else 0)) % 4
            for i in range(3)
        ]
        return device(*place, c)

    copies = {}

    def hop_copy(f, phase, h, axis, src, dst):
        copy = pltpu.make_async_remote_copy(
            src_ref=src, dst_ref=dst, send_sem=gs.at[f, phase, h], recv_sem=gr.at[f, phase, h],
            device_id=there(axis, HOPS[h]), device_id_type=MESH,
        )
        copy.start()
        sends.append(copy)
        copies[f, phase, h] = copy

    def arrived(f, phase):
        for h in range(3):
            copies[f, phase, h].wait_recv()

    def turned(axis, hop, size):
        return pl.multiple_of(((pick(axis, at) + hop) % 4) * size, size)

    for flows in PARTS:
        lo, hi = FLOWS[flows[0]][0], FLOWS[flows[-1]][1]

        def second_half(j, carry):
            rows = pl.ds(pl.multiple_of(256 * j, 256), 256)
            term = part[rows, lo:hi] + nn(a[1, rows, :], r[1, :, lo:hi])
            part[rows, lo:hi] = term
            snd[rows, lo:hi] = term.astype(BF16)
            return carry

        lax.fori_loop(0, 4, second_half, 0)
        for h in range(3):
            for f in flows:
                lo, hi, order = FLOWS[f]
                cols = pl.ds(lo, hi - lo)
                src = snd.at[pl.ds(turned(order[0], HOPS[h], 256), 256), cols]
                hop_copy(f, 0, h, order[0], src, rcv.at[h, :, cols])

    for h in range(2):
        ctx[pl.ds(256 * h, 256), :] = tn(pg[h, 1], v[h]).astype(BF16)

    for flows in PARTS:
        for f in flows:
            lo, hi, order = FLOWS[f]
            cols = pl.ds(lo, hi - lo)
            arrived(f, 0)
            sums = part[pl.ds(turned(order[0], 0, 256), 256), lo:hi]
            for h in range(3):
                sums = sums + rcv[h, :, lo:hi].astype(F32)
            own[:, lo:hi] = sums
            snd2[:, lo:hi] = sums.astype(BF16)
            for h in range(3):
                src = snd2.at[pl.ds(turned(order[1], HOPS[h], 64), 64), cols]
                hop_copy(f, 1, h, order[1], src, rcv2.at[h, :, cols])

    for flows in PARTS:
        for f in flows:
            lo, hi, order = FLOWS[f]
            cols = pl.ds(lo, hi - lo)
            arrived(f, 1)
            sums = own[pl.ds(turned(order[1], 0, 64), 64), lo:hi]
            for h in range(3):
                sums = sums + rcv2[h, :, lo:hi].astype(F32)
            mine = pick(order[2], at)
            last_sums[mine, :, lo:hi] = sums.astype(BF16)
            block = last_sums.at[mine, :, cols]
            for h in range(3):
                hop_copy(f, 2, h, order[2], block, block)

    for flows in PARTS:
        for f in flows:
            lo, hi, order = FLOWS[f]
            arrived(f, 2)
            sums = last_sums[0, :, lo:hi].astype(F32)
            for i in range(1, 4):
                sums = sums + last_sums[i, :, lo:hi].astype(F32)
            first = pick(order[0], at) * 256 + pick(order[1], at) * 64
            rows = pl.ds(pl.multiple_of(first, 64), 64)
            res[c, rows, lo:hi] = sums.astype(BF16)
            block = res.at[c, rows, pl.ds(lo, hi - lo)]
            for h in range(3):
                hop_copy(f, 3, h, order[1], block, block)

    for flows in PARTS:
        for f in flows:
            lo, hi, order = FLOWS[f]
            arrived(f, 3)
            block = res.at[c, pl.ds(turned(order[0], 0, 256), 256), pl.ds(lo, hi - lo)]
            for h in range(3):
                hop_copy(f, 4, h, order[0], block, block)

    forwards = []
    for flows in PARTS:
        for h in (3, 1, 2, 0):
            for f in flows:
                lo, hi, order = FLOWS[f]
                hop = 0
                if h < 3:
                    hop = HOPS[h]
                    copies[f, 4, h].wait_recv()
                block = res.at[c, pl.ds(turned(order[0], 4 - hop, 256), 256), pl.ds(lo, hi - lo)]
                copy = pltpu.make_async_remote_copy(
                    src_ref=block, dst_ref=block, send_sem=fs.at[f, h], recv_sem=fr.at[f, h],
                    device_id=partner, device_id_type=MESH,
                )
                copy.start()
                sends.append(copy)
                forwards.append(copy)
    for copy in forwards:
        copy.wait_recv()
    for copy in sends:
        copy.wait_send()


def finish(sums, context, key_grad, value_grad, context_out, wide, sem):
    copies = [pltpu.make_async_copy(context, context_out, sem.at[8])]
    copies[0].start()
    for i, out in enumerate((key_grad, value_grad)):
        for j in range(4):
            rows = pl.ds(256 * j, 256)
            wide[i, rows, :] = sums[i, rows, :].astype(F32)
            copy = pltpu.make_async_copy(wide.at[i, rows], out.at[rows], sem.at[4 * i + j])
            copy.start()
            copies.append(copy)
    for copy in copies:
        copy.wait()


def body(encoded, queries, cotangent, lengths, key_weight, value_weight):
    any_space = pl.BlockSpec(memory_space=pltpu.HBM)
    dma = pltpu.SemaphoreType.DMA
    grads, context = pl.pallas_call(
        kernel,
        out_shape=(
            pltpu.VMEM((2, 1024, 1024), BF16),
            pltpu.VMEM((512, 1024), BF16),
        ),
        in_specs=[any_space] * 3 + [pl.BlockSpec(memory_space=pltpu.SMEM)] + [any_space] * 2,
        out_specs=(pl.BlockSpec(memory_space=pltpu.VMEM), pl.BlockSpec(memory_space=pltpu.VMEM)),
        scratch_shapes=[
            pltpu.VMEM((2, 80, 8, 1024), BF16),
            pltpu.VMEM((2, 1024, 640), BF16),
            pltpu.VMEM((2, 640, 1024), BF16),
            pltpu.VMEM((2, 640, 256), F32),
            pltpu.VMEM((2, 640, 256), F32),
            pltpu.VMEM((2, 2, 640, 256), BF16),
            pltpu.VMEM((2, 512, 1024), BF16),
            pltpu.VMEM((2, 1024, 1024), BF16),
            pltpu.VMEM((2, 1024, 512), BF16),
            pltpu.VMEM((2, 1024, 256), BF16),
            pltpu.VMEM((2, 512, 1024), BF16),
            pltpu.VMEM((1024, 1024), F32),
            pltpu.VMEM((256, 1024), F32),
            pltpu.VMEM((1024, 1024), BF16),
            pltpu.VMEM((256, 1024), BF16),
            pltpu.VMEM((3, 256, 1024), BF16),
            pltpu.VMEM((3, 64, 1024), BF16),
            pltpu.VMEM((4, 64, 1024), BF16),
            dma((8,)), dma((2, 16)), dma((2, 16)), dma((4,)), dma((4,)),
            dma((6, 5, 3)), dma((6, 5, 3)), dma((6, 4)), dma((6, 4)),
        ],
        compiler_params=pltpu.CompilerParams(
            collective_id=0, has_side_effects=True, vmem_limit_bytes=50 * 2**20
        ),
    )(
        jnp.transpose(encoded, (1, 0, 2)),
        queries.reshape(512, 1024),
        cotangent.reshape(512, 1024),
        lengths,
        key_weight,
        value_weight,
    )
    key_grad, value_grad, context = pl.pallas_call(
        finish,
        out_shape=(
            jax.ShapeDtypeStruct((1024, 1024), F32),
            jax.ShapeDtypeStruct((1024, 1024), F32),
            jax.ShapeDtypeStruct((512, 1024), BF16),
        ),
        in_specs=[pl.BlockSpec(memory_space=pltpu.VMEM)] * 2,
        out_specs=(any_space,) * 3,
        scratch_shapes=[pltpu.VMEM((2, 1024, 1024), F32), dma((9,))],
        compiler_params=pltpu.CompilerParams(vmem_limit_bytes=16 * 2**20),
    )(grads, context)
    return context.reshape(16, 32, 1024), key_grad, value_grad


def solution(mesh):
    return jax.shard_map(
        body,
        mesh=mesh,
        in_specs=(
            P("dp", "tm", None),
            P(("dp", "tm"), None, None),
            P(("dp", "tm"), None, None),
            P(("dp", "tm")),
            P(),
            P(),
        ),
        out_specs=(P(("dp", "tm"), None, None), P(), P()),
        check_vma=False,
    )
```

time: 95.5 us -> 86.4 us (0.905)
  Pallas kernels: 94.8 us -> 85.6 us
    pallas_call x1, Pallas kernels: 91.1 us -> 82 us  [body(): pl.pallas_call(kernel, out_shape=(pltpu.VMEM((2, 1024, 1024), BF16), pltp...]
where the time goes in v3:
time: 86.4 us; the launch traced here: 86.3 us
  Pallas kernels  85.6 us (99%)
    pallas_call x1, Pallas kernels, body(): pl.pallas_call(kernel, out_shape=(pltpu.VMEM((2, 1024, 1024), BF16), pltp...  82 us
    pallas_call x1, Pallas kernels, body(): pl.pallas_call(finish, out_shape=(jax.ShapeDtypeStruct((1024, 1024), F32)...  3.69 us

profile of v3, /device:TPU:1, one launch (start us, length us, event | category | flops | bytes accessed | tf_op | source)
XLA Modules:
  0.0 86.3 jit_solution(10364248221819676822)
XLA Ops:
  0.6 82.0 %shard_map.85 = (bf16[2,1024,1024]{2,1,0:T(8,128)(2,1)S(1)}, bf16[512,1024]{1,0:T(8,128)(2,1)S(1)}) custom-call(bf16[5,256,1024]{2,1,0:T(8,128)(2,1)} %bitcast.4, bf16[512,1024]{1,0:T(8,128)(2,1)} %bitcast.5, bf16[512,1024]{1,0:T(8,128)(2,1)} %bitcast.6, s32[16]{0:T(128)} %lens.1, bf16[1024,1024]{1,0:T(8,128)(2,1)} %wk.1, bf16[1024,1024]{1,0:T(8,128)(2,1)} %wv.1), custom_call_target="tpu_custom_call" | custom-call | tf_op jit(solution)/shard_map/pallas_call | solution.py:344
  82.6 3.7 %shard_map.86 = (f32[1024,1024]{1,0:T(8,128)}, f32[1024,1024]{1,0:T(8,128)}, bf16[512,1024]{1,0:T(8,128)(2,1)}) custom-call(bf16[2,1024,1024]{2,1,0:T(8,128)(2,1)S(1)} %get-tuple-element.8.sums, bf16[512,1024]{1,0:T(8,128)(2,1)S(1)} %get-tuple-element.9.context), custom_call_target="tpu_custom_call" | custom-call | tf_op jit(solution)/shard_map/pallas_call | solution.py:385

commit v4 on v3

--- a/solution.py
+++ b/solution.py
@@ -16,11 +16,17 @@
     (1, 2, 0), (1, 2, 1),
 )
 FLOWS = (
-    (0, 256, (0, 1, 2)), (256, 384, (1, 2, 0)), (384, 512, (2, 0, 1)),
-    (512, 768, (2, 0, 1)), (768, 896, (0, 1, 2)), (896, 1024, (1, 2, 0)),
+    (0, 128, (0, 1, 2), 0, 256), (128, 256, (1, 2, 0), 0, 256),
+    (256, 384, (2, 0, 1), 0, 256), (384, 512, (0, 1, 2), 0, 256),
+    (512, 640, (1, 2, 0), 0, 256), (640, 768, (2, 0, 1), 0, 256),
+    (768, 896, (0, 1, 2), 0, 256),
+    (896, 1024, (1, 2, 0), 0, 128), (896, 1024, (2, 0, 1), 512, 128),
 )
-PARTS = ((0, 1, 2), (3, 4, 5))
+PARTS = ((0, 1), (2, 3), (4, 5), (6, 7, 8))
 HOPS = (2, 1, 3)
+BACK = (0, 1, 2)
+TALL = 1024
+SCHEDULE = ((0, 0), (0, 1), (0, 2), (0, 3), (6, 0)) + tuple((s, p) for s in range(1, 6) for p in range(4))
 
 
 def nt(a, b):
@@ -177,21 +183,26 @@
 
         lax.fori_loop(0, 5, normalise, 0)
 
-    def weigh(h, slot):
+    def weigh(h, slot, rows):
         factor = jnp.where(slot == 0, 1.0 / 32.0, 1.0)
-        return (nn(et[h], pg[h, slot]) * factor).astype(BF16)
+        return (nn(et[h, rows, :], pg[h, slot]) * factor).astype(BF16)
 
     def swap(h):
-        a_out[h] = weigh(h, 1 - c)
-        copy = to_partner(a_out.at[h], a.at[h, :, pl.ds(256, 256)], 2 + h)
-        copy.start()
-        sends.append(copy)
-        a[h, :, 0:256] = weigh(h, c)
-        operands[h].wait_recv()
-        return copy
+        swapped = []
+        for i in range(2):
+            rows = pl.ds(512 * i, 512)
+            a_out[h, rows, :] = weigh(h, 1 - c, rows)
+            copy = to_partner(a_out.at[h, rows], a.at[h, rows, pl.ds(256, 256)], 2 + 2 * h + i)
+            copy.start()
+            sends.append(copy)
+            swapped.append(copy)
+        a[h, :, 0:256] = weigh(h, c, pl.ds(0, 1024))
+        swapped.append(operands[h])
+        return swapped
 
     stream(0)
-    swap(0).wait_recv()
+    for copy in swap(0):
+        copy.wait_recv()
     def first_half(j, carry):
         rows = pl.ds(pl.multiple_of(256 * j, 256), 256)
         part[rows, :] = nn(a[0, rows, :], r[0])
@@ -200,7 +211,8 @@
     lax.fori_loop(0, 4, first_half, 0)
     stream(1)
     last = swap(1)
-    last.wait_recv()
+    for copy in last:
+        copy.wait_recv()
 
     def pick(axis, value):
         return value[axis] * (1 - c) + value[(axis + 1) % 3] * c
@@ -227,97 +239,110 @@
         for h in range(3):
             copies[f, phase, h].wait_recv()
 
-    def turned(axis, hop, size):
-        return pl.multiple_of(((pick(axis, at) + hop) % 4) * size, size)
-
-    for flows in PARTS:
-        lo, hi = FLOWS[flows[0]][0], FLOWS[flows[-1]][1]
+    def turned(axis, hop, size, start=0):
+        return pl.multiple_of(start + ((pick(axis, at) + hop) % 4) * size, size)
+
+    forwards = []
+
+    def own_terms(flows):
+        first, last = FLOWS[flows[0]][0], FLOWS[flows[-1]][1]
 
         def second_half(j, carry):
-            rows = pl.ds(pl.multiple_of(256 * j, 256), 256)
-            term = part[rows, lo:hi] + nn(a[1, rows, :], r[1, :, lo:hi])
-            part[rows, lo:hi] = term
-            snd[rows, lo:hi] = term.astype(BF16)
+            rows = pl.ds(pl.multiple_of(TALL * j, TALL), TALL)
+            term = part[rows, first:last] + nn(a[1, rows, :], r[1, :, first:last])
+            part[rows, first:last] = term
+            snd[rows, first:last] = term.astype(BF16)
             return carry
 
-        lax.fori_loop(0, 4, second_half, 0)
+        lax.fori_loop(0, 1024 // TALL, second_half, 0)
         for h in range(3):
             for f in flows:
-                lo, hi, order = FLOWS[f]
+                lo, hi, order, start, size = FLOWS[f]
                 cols = pl.ds(lo, hi - lo)
-                src = snd.at[pl.ds(turned(order[0], HOPS[h], 256), 256), cols]
-                hop_copy(f, 0, h, order[0], src, rcv.at[h, :, cols])
-
-    for h in range(2):
-        ctx[pl.ds(256 * h, 256), :] = tn(pg[h, 1], v[h]).astype(BF16)
-
-    for flows in PARTS:
+                src = snd.at[pl.ds(turned(order[0], HOPS[h], size, start), size), cols]
+                hop_copy(f, 0, h, order[0], src, rcv.at[h, pl.ds(start // 4, size), cols])
+
+    def second_axis(flows):
         for f in flows:
-            lo, hi, order = FLOWS[f]
+            lo, hi, order, start, size = FLOWS[f]
             cols = pl.ds(lo, hi - lo)
+            base, less = start // 4, size // 4
             arrived(f, 0)
-            sums = part[pl.ds(turned(order[0], 0, 256), 256), lo:hi]
+            sums = part[pl.ds(turned(order[0], 0, size, start), size), lo:hi]
             for h in range(3):
-                sums = sums + rcv[h, :, lo:hi].astype(F32)
-            own[:, lo:hi] = sums
-            snd2[:, lo:hi] = sums.astype(BF16)
+                sums = sums + rcv[h, base : base + size, lo:hi].astype(F32)
+            own[base : base + size, lo:hi] = sums
+            snd2[base : base + size, lo:hi] = sums.astype(BF16)
             for h in range(3):
-                src = snd2.at[pl.ds(turned(order[1], HOPS[h], 64), 64), cols]
-                hop_copy(f, 1, h, order[1], src, rcv2.at[h, :, cols])
-
-    for flows in PARTS:
+                src = snd2.at[pl.ds(turned(order[1], HOPS[h], less, base), less), cols]
+                hop_copy(f, 1, h, order[1], src, rcv2.at[h, pl.ds(start // 16, less), cols])
+
+    def third_axis(flows):
         for f in flows:
-            lo, hi, order = FLOWS[f]
-            cols = pl.ds(lo, hi - lo)
+            lo, hi, order, start, size = FLOWS[f]
+            base, less = start // 16, size // 4
             arrived(f, 1)
-            sums = own[pl.ds(turned(order[1], 0, 64), 64), lo:hi]
+            sums = own[pl.ds(turned(order[1], 0, less, start // 4), less), lo:hi]
             for h in range(3):
-                sums = sums + rcv2[h, :, lo:hi].astype(F32)
+                sums = sums + rcv2[h, base : base + less, lo:hi].astype(F32)
             mine = pick(order[2], at)
-            last_sums[mine, :, lo:hi] = sums.astype(BF16)
-            block = last_sums.at[mine, :, cols]
+            last_sums[mine, base : base + less, lo:hi] = sums.astype(BF16)
+            block = last_sums.at[mine, pl.ds(base, less), pl.ds(lo, hi - lo)]
             for h in range(3):
                 hop_copy(f, 2, h, order[2], block, block)
 
-    for flows in PARTS:
+    def back_second(flows):
         for f in flows:
-            lo, hi, order = FLOWS[f]
+            lo, hi, order, start, size = FLOWS[f]
+            base, less = start // 16, size // 4
             arrived(f, 2)
-            sums = last_sums[0, :, lo:hi].astype(F32)
+            sums = last_sums[0, base : base + less, lo:hi].astype(F32)
             for i in range(1, 4):
-                sums = sums + last_sums[i, :, lo:hi].astype(F32)
-            first = pick(order[0], at) * 256 + pick(order[1], at) * 64
-            rows = pl.ds(pl.multiple_of(first, 64), 64)
+                sums = sums + last_sums[i, base : base + less, lo:hi].astype(F32)
+            first = start + pick(order[0], at) * size + pick(order[1], at) * less
+            rows = pl.ds(pl.multiple_of(first, less), less)
             res[c, rows, lo:hi] = sums.astype(BF16)
             block = res.at[c, rows, pl.ds(lo, hi - lo)]
             for h in range(3):
                 hop_copy(f, 3, h, order[1], block, block)
 
-    for flows in PARTS:
+    def gathered(f, hop):
+        lo, hi, order, start, size = FLOWS[f]
+        return res.at[c, pl.ds(turned(order[0], hop, size, start), size), pl.ds(lo, hi - lo)]
+
+    def forward(f, h):
+        block = gathered(f, 4 - HOPS[h] if h < 3 else 0)
+        copy = pltpu.make_async_remote_copy(
+            src_ref=block, dst_ref=block, send_sem=fs.at[f, h], recv_sem=fr.at[f, h],
+            device_id=partner, device_id_type=MESH,
+        )
+        copy.start()
+        sends.append(copy)
+        forwards.append(copy)
+
+    def back_first(flows):
         for f in flows:
-            lo, hi, order = FLOWS[f]
             arrived(f, 3)
-            block = res.at[c, pl.ds(turned(order[0], 0, 256), 256), pl.ds(lo, hi - lo)]
-            for h in range(3):
-                hop_copy(f, 4, h, order[0], block, block)
-
-    forwards = []
-    for flows in PARTS:
-        for h in (3, 1, 2, 0):
+            block = gathered(f, 0)
+            for h in BACK:
+                hop_copy(f, 4, h, FLOWS[f][2][0], block, block)
+        for f in flows:
+            forward(f, 3)
+
+    def to_other_core(flows):
+        for h in BACK:
             for f in flows:
-                lo, hi, order = FLOWS[f]
-                hop = 0
-                if h < 3:
-                    hop = HOPS[h]
-                    copies[f, 4, h].wait_recv()
-                block = res.at[c, pl.ds(turned(order[0], 4 - hop, 256), 256), pl.ds(lo, hi - lo)]
-                copy = pltpu.make_async_remote_copy(
-                    src_ref=block, dst_ref=block, send_sem=fs.at[f, h], recv_sem=fr.at[f, h],
-                    device_id=partner, device_id_type=MESH,
-                )
-                copy.start()
-                sends.append(copy)
-                forwards.append(copy)
+                copies[f, 4, h].wait_recv()
+                forward(f, h)
+
+    def contexts(flows):
+        for h in range(2):
+            ctx[pl.ds(256 * h, 256), :] = tn(pg[h, 1], v[h]).astype(BF16)
+
+    steps = (own_terms, second_axis, third_axis, back_second, back_first, to_other_core, contexts)
+    for step, p in SCHEDULE:
+        with jax.named_scope(f"s{step}_{p}"):
+            steps[step](PARTS[p])
     for copy in forwards:
         copy.wait_recv()
     for copy in sends:
@@ -368,8 +393,8 @@
             pltpu.VMEM((3, 256, 1024), BF16),
             pltpu.VMEM((3, 64, 1024), BF16),
             pltpu.VMEM((4, 64, 1024), BF16),
-            dma((8,)), dma((2, 16)), dma((2, 16)), dma((4,)), dma((4,)),
-            dma((6, 5, 3)), dma((6, 5, 3)), dma((6, 4)), dma((6, 4)),
+            dma((8,)), dma((2, 16)), dma((2, 16)), dma((6,)), dma((6,)),
+            dma((9, 5, 3)), dma((9, 5, 3)), dma((9, 4)), dma((9, 4)),
         ],
         compiler_params=pltpu.CompilerParams(
             collective_id=0, has_side_effects=True, vmem_limit_bytes=50 * 2**20

time: 86.4 us -> 83.5 us (0.966)
  Pallas kernels: 85.6 us -> 82.7 us
    pallas_call x1, Pallas kernels: 82 us -> 79 us  [body(): pl.pallas_call(kernel, out_shape=(pltpu.VMEM((2, 1024, 1024), BF16), pltp...]
where the time goes in v4:
time: 83.5 us; the launch traced here: 83.4 us
  Pallas kernels  82.7 us (99%)
    pallas_call x1, Pallas kernels, body(): pl.pallas_call(kernel, out_shape=(pltpu.VMEM((2, 1024, 1024), BF16), pltp...  79 us
    pallas_call x1, Pallas kernels, body(): pl.pallas_call(finish, out_shape=(jax.ShapeDtypeStruct((1024, 1024), F32)...  3.69 us

profile of v4, /device:TPU:1, one launch (start us, length us, event | category | flops | bytes accessed | tf_op | source)
XLA Modules:
  0.0 83.4 jit_solution(3597063768941734634)
XLA Ops:
  0.6 79.0 %shard_map.85 = (bf16[2,1024,1024]{2,1,0:T(8,128)(2,1)S(1)}, bf16[512,1024]{1,0:T(8,128)(2,1)S(1)}) custom-call(bf16[5,256,1024]{2,1,0:T(8,128)(2,1)} %bitcast.4, bf16[512,1024]{1,0:T(8,128)(2,1)} %bitcast.5, bf16[512,1024]{1,0:T(8,128)(2,1)} %bitcast.6, s32[16]{0:T(128)} %lens.1, bf16[1024,1024]{1,0:T(8,128)(2,1)} %wk.1, bf16[1024,1024]{1,0:T(8,128)(2,1)} %wv.1), custom_call_target="tpu_custom_call" | custom-call | tf_op jit(solution)/shard_map/pallas_call | solution.py:369
  79.7 3.7 %shard_map.86 = (f32[1024,1024]{1,0:T(8,128)}, f32[1024,1024]{1,0:T(8,128)}, bf16[512,1024]{1,0:T(8,128)(2,1)}) custom-call(bf16[2,1024,1024]{2,1,0:T(8,128)(2,1)S(1)} %get-tuple-element.8.sums, bf16[512,1024]{1,0:T(8,128)(2,1)S(1)} %get-tuple-element.9.context), custom_call_target="tpu_custom_call" | custom-call | tf_op jit(solution)/shard_map/pallas_call | solution.py:410

commit v5 on v4

--- a/solution.py
+++ b/solution.py
@@ -26,7 +26,9 @@
 HOPS = (2, 1, 3)
 BACK = (0, 1, 2)
 TALL = 1024
-SCHEDULE = ((0, 0), (0, 1), (0, 2), (0, 3), (6, 0)) + tuple((s, p) for s in range(1, 6) for p in range(4))
+SCHEDULE = ((0, 0), (0, 1), (0, 2), (0, 3), (6, 0), (7, 0)) + tuple((s, p) for s in range(1, 5) for p in range(4)) + (
+    (7, 0), (5, 0), (5, 1), (5, 2), (5, 3),
+)
 
 
 def nt(a, b):
@@ -255,8 +257,8 @@
             return carry
 
         lax.fori_loop(0, 1024 // TALL, second_half, 0)
-        for h in range(3):
-            for f in flows:
+        for f in flows:
+            for h in range(3):
                 lo, hi, order, start, size = FLOWS[f]
                 cols = pl.ds(lo, hi - lo)
                 src = snd.at[pl.ds(turned(order[0], HOPS[h], size, start), size), cols]
@@ -339,10 +341,21 @@
         for h in range(2):
             ctx[pl.ds(256 * h, 256), :] = tn(pg[h, 1], v[h]).astype(BF16)
 
-    steps = (own_terms, second_axis, third_axis, back_second, back_first, to_other_core, contexts)
+    def drain(flows):
+        done = marks[-4]
+        for copy in sends[:done]:
+            copy.wait_send()
+        del sends[:done]
+        marks[:] = [0] * 4
+
+    marks = [0] * 4
+    steps = (
+        own_terms, second_axis, third_axis, back_second, back_first, to_other_core, contexts, drain,
+    )
     for step, p in SCHEDULE:
-        with jax.named_scope(f"s{step}_{p}"):
-            steps[step](PARTS[p])
+        if step < 7:
+            marks.append(len(sends))
+        steps[step](PARTS[p])
     for copy in forwards:
         copy.wait_recv()
     for copy in sends:

time: 83.5 us -> 83.2 us (level)
  no operation moved by 1% of the time
where the time goes in v5:
time: 83.2 us; the launch traced here: 83.1 us
  Pallas kernels  82.5 us (99%)
    pallas_call x1, Pallas kernels, body(): pl.pallas_call(kernel, out_shape=(pltpu.VMEM((2, 1024, 1024), BF16), pltp...  78.8 us
    pallas_call x1, Pallas kernels, body(): pl.pallas_call(finish, out_shape=(jax.ShapeDtypeStruct((1024, 1024), F32)...  3.69 us

profile of v5, /device:TPU:1, one launch (start us, length us, event | category | flops | bytes accessed | tf_op | source)
XLA Modules:
  0.0 83.1 jit_solution(15165346985108711080)
XLA Ops:
  0.6 78.8 %shard_map.85 = (bf16[2,1024,1024]{2,1,0:T(8,128)(2,1)S(1)}, bf16[512,1024]{1,0:T(8,128)(2,1)S(1)}) custom-call(bf16[5,256,1024]{2,1,0:T(8,128)(2,1)} %bitcast.4, bf16[512,1024]{1,0:T(8,128)(2,1)} %bitcast.5, bf16[512,1024]{1,0:T(8,128)(2,1)} %bitcast.6, s32[16]{0:T(128)} %lens.1, bf16[1024,1024]{1,0:T(8,128)(2,1)} %wk.1, bf16[1024,1024]{1,0:T(8,128)(2,1)} %wv.1), custom_call_target="tpu_custom_call" | custom-call | tf_op jit(solution)/shard_map/pallas_call | solution.py:382
  79.4 3.7 %shard_map.86 = (f32[1024,1024]{1,0:T(8,128)}, f32[1024,1024]{1,0:T(8,128)}, bf16[512,1024]{1,0:T(8,128)(2,1)}) custom-call(bf16[2,1024,1024]{2,1,0:T(8,128)(2,1)S(1)} %get-tuple-element.8.sums, bf16[512,1024]{1,0:T(8,128)(2,1)S(1)} %get-tuple-element.9.context), custom_call_target="tpu_custom_call" | custom-call | tf_op jit(solution)/shard_map/pallas_call | solution.py:423

commit v6 on v5

--- a/solution.py
+++ b/solution.py
@@ -45,7 +45,7 @@
 
 def kernel(
     enc, q, cot, lens, wk, wv, res, ctx,
-    e, et, v, st, gp, pg, qc, w, a, a_out, r, part, own, snd, snd2, rcv, rcv2, last_sums,
+    es, e, et, v, st, gp, pg, qc, w, a, a_out, r, part, own, snd, snd2, rcv, rcv2, last_sums,
     lsem, xs, xr, ds, dr, gs, gr, fs, fr,
 ):
     tm, dp = lax.axis_index("tm"), lax.axis_index("dp")
@@ -66,17 +66,13 @@
 
     partner = device(x, y, z, 1 - c)
 
+    load = pltpu.make_async_copy(enc, es, lsem.at[4])
+    load.start()
     local = [
         pltpu.make_async_copy(q, qc.at[0], lsem.at[0]),
         pltpu.make_async_copy(cot, qc.at[1], lsem.at[1]),
         pltpu.make_async_copy(wk, w.at[0], lsem.at[2]),
         pltpu.make_async_copy(wv, w.at[1], lsem.at[3]),
-        pltpu.make_async_copy(
-            enc.at[:, pl.ds(pl.multiple_of(16 * tm, 16), 8)], e.at[0, pl.ds(0, 5)], lsem.at[4]
-        ),
-        pltpu.make_async_copy(
-            enc.at[:, pl.ds(pl.multiple_of(16 * tm + 8, 8), 8)], e.at[1, pl.ds(0, 5)], lsem.at[5]
-        ),
     ]
     barrier = pltpu.get_barrier_semaphore()
     peers = [(tm_at(off, 1), dp) for off in OFFS[1:]]
@@ -85,11 +81,17 @@
         pl.semaphore_signal(barrier, inc=1, device_id=peer, device_id_type=MESH)
     for copy in local:
         copy.start()
+    load.wait()
+    for h in range(2):
+        rows = pl.ds(pl.multiple_of(16 * tm + 8 * h, 8), 8)
+        copy = pltpu.make_async_copy(es.at[:, rows], e.at[h, pl.ds(0, 5)], lsem.at[5 + 3 * h])
+        copy.start()
+        local.append(copy)
     pl.semaphore_wait(barrier, len(peers))
 
     def exchange(h, k, target):
         return pltpu.make_async_remote_copy(
-            src_ref=enc.at[:, pl.ds(pl.multiple_of(16 * target + 8 * h, 8), 8)],
+            src_ref=es.at[:, pl.ds(pl.multiple_of(16 * target + 8 * h, 8), 8)],
             dst_ref=e.at[h, pl.ds(5 * k, 5)],
             send_sem=xs.at[h, k],
             recv_sem=xr.at[h, k],
@@ -144,7 +146,7 @@
             for i in range(3):
                 k = 3 * j + 1 + i
                 pltpu.make_async_remote_copy(
-                    src_ref=enc.at[:, pl.ds(0, 8)],
+                    src_ref=es.at[:, pl.ds(0, 8)],
                     dst_ref=e.at[h, pl.ds(5 * k, 5)],
                     send_sem=xs.at[h, k],
                     recv_sem=xr.at[h, k],
@@ -388,6 +390,7 @@
         in_specs=[any_space] * 3 + [pl.BlockSpec(memory_space=pltpu.SMEM)] + [any_space] * 2,
         out_specs=(pl.BlockSpec(memory_space=pltpu.VMEM), pl.BlockSpec(memory_space=pltpu.VMEM)),
         scratch_shapes=[
+            pltpu.VMEM((5, 256, 1024), BF16),
             pltpu.VMEM((2, 80, 8, 1024), BF16),
             pltpu.VMEM((2, 1024, 640), BF16),
             pltpu.VMEM((2, 640, 1024), BF16),
@@ -406,7 +409,7 @@
             pltpu.VMEM((3, 256, 1024), BF16),
             pltpu.VMEM((3, 64, 1024), BF16),
             pltpu.VMEM((4, 64, 1024), BF16),
-            dma((8,)), dma((2, 16)), dma((2, 16)), dma((6,)), dma((6,)),
+            dma((9,)), dma((2, 16)), dma((2, 16)), dma((6,)), dma((6,)),
             dma((9, 5, 3)), dma((9, 5, 3)), dma((9, 4)), dma((9, 4)),
         ],
         compiler_params=pltpu.CompilerParams(

time: 83.2 us -> 83 us (level)
  no operation moved by 1% of the time
where the time goes in v6:
time: 83 us; the launch traced here: 82.9 us
  Pallas kernels  82.2 us (99%)
    pallas_call x1, Pallas kernels, body(): pl.pallas_call(kernel, out_shape=(pltpu.VMEM((2, 1024, 1024), BF16), pltp...  78.5 us
    pallas_call x1, Pallas kernels, body(): pl.pallas_call(finish, out_shape=(jax.ShapeDtypeStruct((1024, 1024), F32)...  3.69 us

profile of v6, /device:TPU:1, one launch (start us, length us, event | category | flops | bytes accessed | tf_op | source)
XLA Modules:
  0.0 82.9 jit_solution(16009661401304136467)
XLA Ops:
  0.6 78.5 %shard_map.85 = (bf16[2,1024,1024]{2,1,0:T(8,128)(2,1)S(1)}, bf16[512,1024]{1,0:T(8,128)(2,1)S(1)}) custom-call(bf16[5,256,1024]{2,1,0:T(8,128)(2,1)} %bitcast.4, bf16[512,1024]{1,0:T(8,128)(2,1)} %bitcast.5, bf16[512,1024]{1,0:T(8,128)(2,1)} %bitcast.6, s32[16]{0:T(128)} %lens.1, bf16[1024,1024]{1,0:T(8,128)(2,1)} %wk.1, bf16[1024,1024]{1,0:T(8,128)(2,1)} %wv.1), custom_call_target="tpu_custom_call" | custom-call | tf_op jit(solution)/shard_map/pallas_call | solution.py:384
  79.2 3.7 %shard_map.86 = (f32[1024,1024]{1,0:T(8,128)}, f32[1024,1024]{1,0:T(8,128)}, bf16[512,1024]{1,0:T(8,128)(2,1)}) custom-call(bf16[2,1024,1024]{2,1,0:T(8,128)(2,1)S(1)} %get-tuple-element.8.sums, bf16[512,1024]{1,0:T(8,128)(2,1)S(1)} %get-tuple-element.9.context), custom_call_target="tpu_custom_call" | custom-call | tf_op jit(solution)/shard_map/pallas_call | solution.py:426
